TPU v7x, 256 devices: a whole 4x4x8 slice. The times are simulated.
256 devices in a mesh: rep: 32 (over x, z_lo, core), fsdp: 8 (over z_hi, y).
Axes of the slice: x: 4, y: 4, z: 8 (z_hi: 2, z_lo: 4; z = z_hi * 4 + z_lo), core: 2. Of those that a mesh axis runs over, the one named last changes fastest.
Arguments:
- hidden: bfloat16 [32768, 8192], P(('rep', 'fsdp')), may hold values from -6 to 6
- local_weight: bfloat16 [32, 8192, 2048], P('rep', 'fsdp'), may hold values from -0.125 to 0.125
- master: float32 [8192, 2048], P('fsdp', 'rep'), may hold values from -0.0625 to 0.0625
- momentum: float32 [8192, 2048], P('fsdp', 'rep'), may hold values from -0.06 to 0.06
- dither: int32 [32, 8192, 16], P('rep', 'fsdp'), may hold values from 0 to 15
Outputs:
- key_values: bfloat16 [32768, 2048], P(('rep', 'fsdp'))
- new_master: float32 [8192, 2048], P('fsdp', 'rep')
- new_momentum: float32 [8192, 2048], P('fsdp', 'rep')
- new_local: bfloat16 [32, 8192, 2048], P('rep', 'fsdp')
All inputs are finite; a program needn't handle non-finite values.
Results may differ from a plain program's by a relative error of at most 0.0067.
Values may be sent and summed in bfloat16 or wider, within the bound.
A program may use at most 192 MiB of HBM per device.

v0:
```python
import math

import jax
import jax.numpy as jnp
from jax import lax
from jax.sharding import Mesh
from jax.sharding import PartitionSpec as P

BLOCK = 128
FSDP = ("fsdp_0", "fsdp_1")
REP = ("rep_0", "rep_1", "rep_2")
REP_FSDP = ("rep_0", "rep_1", "rep_2", "fsdp_0", "fsdp_1")


momentum_keep = 0.9
outer_rate = 0.7
mix_share = 0.5


def in_order(parts, dim):
    lengths = list(parts.shape[1:])
    lengths[dim] *= parts.shape[0]
    return jnp.moveaxis(parts, 0, dim).reshape(lengths)


def stacked_from(shard, axes, order):
    parts = shard[None]
    for k in order:
        parts = lax.all_gather(parts, axes[k], axis=0, tiled=True)
    carried = [lax.axis_size(axes[k]) for k in reversed(order)]
    parts = parts.reshape(*carried, *shard.shape)
    turned = sorted(range(len(order)), key=lambda place: order[len(order) - 1 - place])
    return parts.transpose(*turned, *range(len(order), parts.ndim)).reshape(-1, *shard.shape)


def gathered_by_axis(shard, axes, order, dim):
    return in_order(stacked_from(shard, axes, order), dim)


def sent_to_all(shard, axis):
    copies = jnp.broadcast_to(shard, (lax.axis_size(axis), *shard.shape))
    return lax.all_to_all(copies, axis, split_axis=0, concat_axis=0, tiled=True)


def whole_of(shard, axes, dim):
    far, near = axes
    parts = sent_to_all(sent_to_all(shard, far), near)
    return in_order(parts.swapaxes(0, 1).reshape(-1, *shard.shape), dim)


def code_block(delta, dither):
    row_count = delta.shape[0]
    blocked = delta.reshape(row_count, -1, BLOCK)
    scaling = (jnp.max(jnp.abs(blocked), axis=2, keepdims=True) + 1e-06) / 7.0
    offset = (dither.astype(jnp.float32)[:, :, None] + 0.5) / 16.0 - 0.5
    levels = jnp.clip(blocked / scaling + offset, -8.0, 7.0)
    smooth = levels - jnp.sin(2.0 * math.pi * levels) / (2.0 * math.pi)
    return (scaling * (smooth - offset)).reshape(row_count, -1)


def shards(hidden, local_weight, master, momentum, dither):
    weights = local_weight[0]
    local_rows = weights.shape[0]
    key_values = jnp.dot(
        hidden, gathered_by_axis(weights, FSDP, (0, 1), 0), preferred_element_type=jnp.float32
    ).astype(jnp.bfloat16)
    anchor = whole_of(master.astype(jnp.bfloat16), (("rep_0", "rep_1"), "rep_2"), 1)
    delta = anchor.astype(jnp.float32) - weights.astype(jnp.float32)
    coded = code_block(delta, dither[0]).astype(jnp.bfloat16)
    replicas = lax.axis_size(REP)
    received = lax.all_to_all(coded, REP, split_axis=1, concat_axis=0, tiled=True)
    summed = jnp.sum(received.reshape(replicas, local_rows, -1).astype(jnp.float32), axis=0)
    averaged = summed / replicas
    new_momentum = momentum_keep * momentum + averaged
    new_master = master - outer_rate * (averaged + momentum_keep * new_momentum)
    gathered = whole_of(new_master.astype(jnp.bfloat16), (("rep_0", "rep_1"), "rep_2"), 1)
    merged = mix_share * weights.astype(jnp.float32) + (1.0 - mix_share) * gathered.astype(
        jnp.float32
    )
    new_local = merged.astype(jnp.bfloat16)[None]
    return (key_values, new_master, new_momentum, new_local)


def solution(mesh):
    finer = Mesh(
        mesh.devices.reshape(4, 4, 2, 2, 4), ("rep_0", "rep_1", "rep_2", "fsdp_0", "fsdp_1")
    )
    in_specs = (
        P(REP_FSDP, None),
        P(REP, FSDP, None),
        P(FSDP, REP),
        P(FSDP, REP),
        P(REP, FSDP, None),
    )
    out_specs = (P(REP_FSDP, None), P(FSDP, REP), P(FSDP, REP), P(REP, FSDP, None))
    return jax.shard_map(
        shards, mesh=finer, in_specs=in_specs, out_specs=out_specs, check_vma=False
    )
```

profile of v0, /device:TPU:41, one launch (start us, length us, event | category | flops | bytes accessed | tf_op | source)
XLA Modules:
  0.0 557.5 jit_solution(13322060430235633320)
XLA Ops:
  7.2 0.0 copy-start
  7.2 0.0 copy-start.3
  7.2 0.0 all-gather.3.cloned.1.call-start
  7.2 0.7 all-gather.3.cloned.1.call-update
  7.9 0.0 all-gather.5.cloned.1.call-start
  8.0 206.7 %all-gather.3.cloned.1.call-done = bf16[2,1024,2048]{2,1,0:T(8,128)(2,1)} async-done(((bf16[1,1024,2048]{2,1,0:T(8,128)(2,1)}), bf16[2,1024,2048]{2,1,0:T(8,128)(2,1)}) %all-gather.3.cloned.1.call-update) | async-done | bytes 8388624 | tf_op jit(solution)/shard_map/all_gather | solution.py:29
  214.6 0.0 all-gather.5.cloned.1.call-update
  214.6 0.0 copy-done.3
  214.7 0.0 copy-start.5
  214.7 1.6 broadcast_in_dim.15
  216.3 6.6 %all-to-all-start = ((bf16[16,1024,64]{1,2,0:T(8,128)(2,1)}), bf16[16,1024,64]{1,2,0:T(8,128)(2,1)}, u32[]{:S(2)}, u32[]{:S(2)}) async-start(bf16[16,1024,64]{1,2,0:T(8,128)(2,1)} %broadcast_in_dim.15), calls=%async_computation | async-start | bytes 4194304 | tf_op jit(solution)/shard_map/all_to_all | solution.py:42
  222.9 6.5 %copy.19 = bf16[1,1024,2048]{1,2,0:T(8,128)(2,1)} copy(bf16[1,1024,2048]{2,1,0:T(8,128)(2,1)} %param.6) | data formatting | bytes 8388608 | tf_op args[1]
  229.4 0.0 copy-done.5
  229.4 0.1 add.56
  229.5 39.9 %all-to-all-done = bf16[16,1024,64]{1,2,0:T(8,128)(2,1)} async-done(((bf16[16,1024,64]{1,2,0:T(8,128)(2,1)}), bf16[16,1024,64]{1,2,0:T(8,128)(2,1)}, u32[]{:S(2)}, u32[]{:S(2)}) %all-to-all-start) | async-done | bytes 2097184 | tf_op jit(solution)/shard_map/all_to_all | solution.py:42
  269.5 2.2 broadcast_in_dim.16
  271.6 7.2 %all_to_all.30 = bf16[2,16,1024,64]{2,3,1,0:T(8,128)(2,1)S(1)} all-to-all(bf16[2,16,1024,64]{2,3,1,0:T(8,128)(2,1)S(1)} %broadcast_in_dim.16), channel_id=1, replica_groups=mesh['rep_0'=4,'rep_1'=4,'rep_2'=2,'fsdp_0'=2,'fsdp_1'=4] {'rep_2'}, dimensions={0} | all-to-all | bytes 8388608 | tf_op jit(solution)/shard_map/all_to_all | solution.py:42
  278.9 1.0 convert_bitcast_fusion.1
  279.9 0.8 copy.18
  280.8 0.0 copy-start.1
  280.8 9.9 %abs_reduce_fusion = (f32[1024,32]{0,1:T(8,128)S(1)}, f32[1024,32,64]{0,2,1:T(8,128)}) fusion(f32[16,2,1024,64]{2,3,1,0:T(8,128)S(1)} %copy.18, bf16[1024,32,64]{0,2,1:T(8,128)(2,1)} %bitcast.34), kind=kLoop, calls=%fused_computation.6 | loop fusion | flops 8355840 | bytes 21102592 | tf_op jit(solution)/shard_map/reduce_max | solution.py:54
  290.7 0.0 copy-done.1
  290.7 0.1 reduce_max.14
  290.8 0.2 reduce_max.18
  291.0 0.1 mul.36
  291.1 31.6 %multiply_convert_fusion.1 = bf16[1024,32,64]{0,2,1:T(8,128)(2,1)S(1)} fusion(f32[1024,32]{0,1:T(8,128)S(1)} %add.56, f32[1024,32]{0,1:T(8,128)S(1)} %mul.36, f32[1024,32,64]{0,2,1:T(8,128)} %get-tuple-element.20, f32[16,2,1024,64]{2,3,1,0:T(8,128)} %copy-done.1), kind=kLoop, calls=%fused_computation.5 | loop fusion | flops 20971520 | bytes 21233664 | tf_op jit(solution)/shard_map/convert_element_type | solution.py:69
  322.7 0.0 copy-start.4
  322.7 100.0 %all_to_all.31 = bf16[1024,32,64]{0,2,1:T(8,128)(2,1)S(1)} all-to-all(bf16[1024,32,64]{0,2,1:T(8,128)(2,1)S(1)} %multiply_convert_fusion.1), channel_id=1, replica_groups=mesh['rep_0'=4,'rep_1'=4,'rep_2'=2,'fsdp_0'=2,'fsdp_1'=4] {'rep_0','rep_..., dimensions={1} | all-to-all | bytes 8388608 | tf_op jit(solution)/shard_map/all_to_all | solution.py:71
  422.7 0.9 convert_reduce_fusion
  423.7 0.0 copy-done.4
  423.7 0.9 fusion
  424.6 0.2 broadcast_in_dim.17
  424.8 52.9 %all_to_all.32 = bf16[16,1024,64]{1,2,0:T(8,128)(2,1)S(1)} all-to-all(bf16[16,1024,64]{1,2,0:T(8,128)(2,1)S(1)} %broadcast_in_dim.17), channel_id=1, replica_groups=mesh['rep_0'=4,'rep_1'=4,'rep_2'=2,'fsdp_0'=2,'fsdp_1'=4] {'rep_0','rep_1'}, dimensions={0} | all-to-all | bytes 4194304 | tf_op jit(solution)/shard_map/all_to_all | solution.py:42
  477.7 0.6 broadcast_in_dim.18
  478.3 9.5 %all_to_all.33 = bf16[2,16,1024,64]{2,3,1,0:T(8,128)(2,1)S(1)} all-to-all(bf16[2,16,1024,64]{2,3,1,0:T(8,128)(2,1)S(1)} %broadcast_in_dim.18), channel_id=1, replica_groups=mesh['rep_0'=4,'rep_1'=4,'rep_2'=2,'fsdp_0'=2,'fsdp_1'=4] {'rep_2'}, dimensions={0} | all-to-all | bytes 8388608 | tf_op jit(solution)/shard_map/all_to_all | solution.py:42
  487.8 4.3 convert_bitcast_fusion
  492.1 0.0 copy-start.2
  492.1 8.4 %copy.20 = f32[16,2,1024,64]{2,3,1,0:T(8,128)} copy(f32[16,2,1024,64]{2,3,0,1:T(8,128)} %convert_bitcast_fusion) | data formatting | bytes 16777216 | tf_op jit(solution)/shard_map/convert_element_type | solution.py:77
  500.5 0.0 copy-done.2
  500.5 7.1 %multiply_convert_fusion = bf16[1,1024,2048]{1,2,0:T(8,128)(2,1)} fusion(f32[1,1024,2048]{1,2,0:T(8,128)} %bitcast.36, bf16[1,1024,2048]{1,2,0:T(8,128)(2,1)S(1)} %copy-done.2), kind=kLoop, calls=%fused_computation.3 | loop fusion | flops 8388608 | bytes 16777216 | tf_op jit(solution)/shard_map/convert_element_type | solution.py:80
  507.5 6.4 %copy.21 = bf16[1,1024,2048]{2,1,0:T(8,128)(2,1)} copy(bf16[1,1024,2048]{1,2,0:T(8,128)(2,1)} %multiply_convert_fusion) | data formatting | bytes 8388608
  513.9 0.0 all-gather.5.cloned.1.call-done
  513.9 23.0 %copy.17 = bf16[2,4,1024,2048]{3,2,1,0:T(8,128)(2,1)} copy(bf16[2,4,1024,2048]{3,2,0,1:T(8,128)(2,1)} %bitcast.35) | data formatting | bytes 67108864 | tf_op jit(solution)/shard_map/transpose | solution.py:33
  536.9 0.0 copy-done
  536.9 13.7 %convolution_convert_fusion = bf16[128,2048]{1,0:T(8,128)(2,1)} fusion(bf16[128,8192]{1,0:T(8,128)(2,1)S(1)} %copy-done, bf16[8192,2048]{1,0:T(8,128)(2,1)} %bitcast.33), kind=kOutput, calls=%fused_computation.7 | convolution fusion | flops 4295229440 | bytes 36175872 | tf_op jit(solution)/shard_map/dot_general | solution.py:64
  (5 shorter events, 0.1 us)
Async XLA Ops:
  7.2 529.7 %copy-start = (bf16[128,8192]{1,0:T(8,128)(2,1)S(1)}, bf16[128,8192]{1,0:T(8,128)(2,1)}, u32[]{:S(2)}) copy-start(bf16[128,8192]{1,0:T(8,128)(2,1)} %param.5) | copy-start | bytes 6291460
  7.2 207.5 %copy-start.3 = (f32[1024,64]{0,1:T(8,128)S(1)}, f32[1024,64]{0,1:T(8,128)}, u32[]{:S(2)}) copy-start(f32[1024,64]{0,1:T(8,128)} %param.7) | copy-start | bytes 786436
  7.2 207.4 %all-gather.3.cloned.1.call-start = ((), (), s32[]{:S(2)}) async-start(), calls=%async_computation.5 | async-start | bytes 12582912 | tf_op jit(solution)/shard_map/all_gather | solution.py:29
  7.9 506.0 %all-gather.5.cloned.1.call-start = ((), (), s32[]{:S(2)}) async-start(), calls=%async_computation.6 | async-start | bytes 41943040 | tf_op jit(solution)/shard_map/all_gather | solution.py:29
  214.7 14.7 %copy-start.5 = (s32[1,1024,16]{1,2,0:T(8,128)S(1)}, s32[1,1024,16]{1,2,0:T(8,128)}, u32[]{:S(2)}) copy-start(s32[1,1024,16]{1,2,0:T(8,128)} %param.9) | copy-start | bytes 196612
  216.3 53.2 %all-to-all-start = ((bf16[16,1024,64]{1,2,0:T(8,128)(2,1)}), bf16[16,1024,64]{1,2,0:T(8,128)(2,1)}, u32[]{:S(2)}, u32[]{:S(2)}) async-start(bf16[16,1024,64]{1,2,0:T(8,128)(2,1)} %broadcast_in_dim.15), calls=%async_computation | async-start | bytes 4194304 | tf_op jit(solution)/shard_map/all_to_all | solution.py:42
  280.8 9.9 %copy-start.1 = (f32[16,2,1024,64]{2,3,1,0:T(8,128)}, f32[16,2,1024,64]{2,3,1,0:T(8,128)S(1)}, u32[]{:S(2)}) copy-start(f32[16,2,1024,64]{2,3,1,0:T(8,128)S(1)} %copy.18) | copy-start | bytes 25165828
  322.7 101.0 %copy-start.4 = (f32[1024,64]{0,1:T(8,128)S(1)}, f32[1024,64]{0,1:T(8,128)}, u32[]{:S(2)}) copy-start(f32[1024,64]{0,1:T(8,128)} %param.8) | copy-start | bytes 786436
  492.1 8.4 %copy-start.2 = (bf16[1,1024,2048]{1,2,0:T(8,128)(2,1)S(1)}, bf16[1,1024,2048]{1,2,0:T(8,128)(2,1)}, u32[]{:S(2)}) copy-start(bf16[1,1024,2048]{1,2,0:T(8,128)(2,1)} %copy.19) | copy-start | bytes 12582916
Sparse Core Ops, SparseCore 0:
  9.8 204.7 all-gather.2
  216.4 294.8 all-gather.4
where the time goes:
time: 561 us; the launch traced here: 557 us
  waiting for transfers between devices  247 us (44%)
  blocking collectives  170 us (30%)
  other arithmetic  55.9 us (10%)
  local copies, waits for them, and re-layouts  50.1 us (9%)
  between operations  14.2 us (3%)
  matrix products  13.7 us (2%)
  starting transfers between devices  6.71 us (1%)
    all_gather x2, waiting for transfers between devices, stacked_from(): parts = lax.all_gather(parts, axes[k], axis=0, tiled=True)  207 us
    all_to_all x1, blocking collectives, shards(): lax.all_to_all(coded, REP, split_axis=1, concat_axis=0, tiled=True)  100 us
    all_to_all x3, blocking collectives, sent_to_all(): return lax.all_to_all(copies, axis, split_axis=0, concat_axis=0, tiled=True)  69.5 us
    all_to_all x1, waiting for transfers between devices, sent_to_all(): return lax.all_to_all(copies, axis, split_axis=0, concat_axis=0, tiled=True)  39.9 us
    convert_element_type x1, other arithmetic, shards(): coded = code_block(delta, dither[0]).astype(jnp.bfloat16)  31.6 us
    transpose x1, local copies, waits for them, and re-layouts, stacked_from(): parts.transpose(*turned, *range(len(order), parts.ndim))  23 us
    dot_general x1, matrix products, shards(): jnp.dot(hidden, gathered_by_axis(weights, FSDP, (0, 1), 0), preferred_ele...  13.7 us
    unnamed x14, local copies, waits for them, and re-layouts  12.9 us
  transfers between devices with their start and end apart: 3, of which 2 were waited for; matrix products, arithmetic and copies ran while one was open for 15% of the time, Pallas kernels for 0%

commit v1 on v0

v1 whole, which is shorter than its diff:
```python
import functools

import jax
import jax.numpy as jnp
from jax import lax
from jax.experimental import pallas as pl
from jax.experimental.pallas import tpu as pltpu
from jax.sharding import Mesh
from jax.sharding import PartitionSpec as P

BLOCK = 128
FSDP = ("zh", "y")
REP = ("x", "z", "c")
REP_FSDP = ("x", "z", "c", "zh", "y")
MESH = pl.DeviceIdType.MESH

momentum_keep = 0.9
outer_rate = 0.7
mix_share = 0.5

NC = 2
F32 = jnp.float32
BF16 = jnp.bfloat16

SINC = (0.9999999993, -6.579735975, 12.98786004, -12.20766404, 6.688634018, -2.371384249, 0.5153655921)


def sine_share(levels):
    turn = levels - jnp.round(levels)
    square = turn * turn
    series = jnp.full_like(square, SINC[-1])
    for coefficient in SINC[-2::-1]:
        series = series * square + coefficient
    return turn * series


def kernel(
    hidden, weights, dither, master, momentum,
    key_values, new_master, new_momentum, new_local,
    wv, dv, mas, mom, mas_in, mom_in, nmas, nmom, held, coded, paired, rx1, rx2, rz, fresh, merged,
    hr, ps1, pr1, ps2, pr2, psz, prz, kept, kv,
    send_sem, recv_sem, local_sem,
):
    rows, columns = wv.shape
    blocks = columns // BLOCK
    groups, _, rc, _ = held.shape
    x, z, c = lax.axis_index("x"), lax.axis_index("z"), lax.axis_index("c")
    zh, y = lax.axis_index("zh"), lax.axis_index("y")

    def flips(i):
        return i, i + 1 - 2 * lax.rem(i, 2), lax.rem(i + 2, 4), 3 - i

    xs, zs, ys = flips(x), flips(z), flips(y)
    x1, x3 = xs[1], xs[3]
    mine = x * 4 + z
    pair = lax.div(x, 2)

    counts = {"remote": 0, "local": 0}
    sends = []
    puts = []

    def remote(src, dst, target):
        i = counts["remote"]
        counts["remote"] += 1
        copy = pltpu.make_async_remote_copy(
            src_ref=src, dst_ref=dst, send_sem=send_sem.at[i], recv_sem=recv_sem.at[i],
            device_id=target, device_id_type=MESH,
        )
        copy.start()
        sends.append(copy)
        return copy

    def local(src, dst):
        i = counts["local"]
        counts["local"] += 1
        copy = pltpu.make_async_copy(src, dst, local_sem.at[i])
        copy.start()
        return copy

    in_master = local(master, mas)
    in_weights = local(weights, wv)
    in_dither = local(dither, dv)
    in_momentum = local(momentum, mom)
    depth = hr.shape[3]
    own_columns = pl.ds(pl.multiple_of((zh * 4 + y) * depth, depth), depth)
    in_hidden = local(hidden.at[:, own_columns], hr.at[0, 0])

    barrier = pltpu.get_barrier_semaphore()
    peers = [{"c": 1 - c}, {"x": x1}, {"x": x3}]
    peers += [{"z": zs[d]} for d in (1, 2, 3)]
    peers += [{"y": ys[d]} for d in (1, 2, 3)]
    peers += [{"zh": 1 - zh, "y": ys[d]} for d in range(4)]
    for peer in peers:
        pl.semaphore_signal(barrier, inc=1, device_id=peer, device_id_type=MESH)
    pl.semaphore_wait(barrier, len(peers))

    half_rows = rows // 2
    my_rows = pl.ds(pl.multiple_of(c * half_rows, half_rows), half_rows)
    other_rows = pl.ds(pl.multiple_of((1 - c) * half_rows, half_rows), half_rows)
    in_master.wait()
    got_master = remote(mas.at[other_rows], mas_in, {"c": 1 - c})

    def first_group(half, k):
        return (half * NC + k) * 2

    def group_rows(group):
        return pl.multiple_of(group * rc, rc)

    def gather_start(buffer, k):
        g = first_group(c, k)
        piece = buffer.at[pl.ds(g, 2), mine]
        over_z = [remote(piece, piece, {"z": zs[d]}) for d in (1, 2, 3)]
        return over_z

    def gather(buffer, k, over_z, times):
        g = first_group(c, k)
        partner = {"c": 1 - c}

        def pass_on(part):
            return remote(part, part, partner)

        def part(ab, first, count):
            return buffer.at[g + ab, pl.ds(first, count)]

        yield times[0]
        for copy in over_z:
            copy.wait_recv()
        own_a, own_b = part(0, 4 * x, 4), part(1, 4 * x, 4)
        a1 = remote(own_a, own_a, {"x": x1})
        b1 = remote(own_b, own_b, {"x": x3})
        b2 = remote(own_b, own_b, {"x": x1})
        a2 = remote(own_a, own_a, {"x": x3})
        passed = [pass_on(buffer.at[pl.ds(g, 2), pl.ds(4 * x, 4)])]
        yield times[1]
        a1.wait_recv()
        far_a = part(0, 4 * x1, 4)
        a3 = remote(far_a, far_a, {"x": x3})
        passed.append(pass_on(far_a))
        b1.wait_recv()
        far_b = part(1, 4 * x3, 4)
        b3 = remote(far_b, far_b, {"x": x1})
        passed.append(pass_on(far_b))
        yield times[2]
        b2.wait_recv()
        passed.append(pass_on(part(1, 4 * x1, 4)))
        a2.wait_recv()
        passed.append(pass_on(part(0, 4 * x3, 4)))
        a3.wait_recv()
        passed.append(pass_on(part(0, 4 * xs[2], 4)))
        b3.wait_recv()
        passed.append(pass_on(part(1, 4 * xs[2], 4)))
        yield times[3]
        for copy in passed:
            copy.wait_recv()

    tile = 16

    def code_groups(first, count):
        start = group_rows(first)

        @pl.loop(0, count * rc // tile)
        def _(i):
            at = pl.multiple_of(start + i * tile, tile)
            group = first + lax.div(i, rc // tile)
            inner = pl.multiple_of(lax.rem(i, rc // tile) * tile, tile)
            here = pl.ds(inner, tile)
            offsets = (dv[pl.ds(at, tile), :].astype(F32) + 0.5) / 16.0 - 0.5
            for b in range(blocks):
                old = wv[pl.ds(at, tile), b * BLOCK:(b + 1) * BLOCK].astype(F32)
                delta = held[group, b, here, :].astype(F32) - old
                largest = jnp.max(jnp.abs(delta), axis=1, keepdims=True)
                scaling = (largest + 1e-06) / 7.0
                offset = offsets[:, b:b + 1]
                levels = jnp.clip(delta * (1.0 / scaling) + offset, -8.0, 7.0)
                smooth = levels - sine_share(levels)
                coded[group, b, here, :] = (scaling * (smooth - offset)).astype(BF16)

    def add_into(target, source):
        step = 64 if rc % 64 == 0 else rc
        n = source.shape[0]

        @pl.loop(0, n * (rc // step))
        def _(i):
            at = (lax.div(i, rc // step), pl.ds(pl.multiple_of(lax.rem(i, rc // step) * step, step), step))
            target[at] = (target[at].astype(F32) + source[at].astype(F32)).astype(BF16)

    def chunk(k, times):
        g, other = first_group(c, k), first_group(1 - c, k)
        times = iter(times)
        yield from gather(held, k, anchors[k], [next(times) for _ in range(4)])
        code_groups(other, 2)
        got = remote(coded.at[pl.ds(other, 2)], paired.at[k], {"c": 1 - c})
        code_groups(g, 2)
        yield next(times)
        got.wait_recv()
        ga, gb = g, g + 1

        def spot(group, first, count):
            return coded.at[group, pl.ds(first, count)]

        def take(ab, first, count):
            add_into(spot(g + ab, first, count), paired.at[k, ab, pl.ds(first, count)])

        away = 8 * (1 - pair)
        take(0, away, 8)
        a1 = remote(spot(ga, away, 8), rx1.at[k, 0], {"x": x3})
        take(1, 4 * x1, 4)
        b1 = remote(spot(gb, 4 * x1, 4), rx1.at[k, 1, pl.ds(0, 4)], {"x": x1})
        take(1, 4 * xs[2], 4)
        b2 = remote(spot(gb, 4 * xs[2], 4), rx1.at[k, 1, pl.ds(4, 4)], {"x": x1})
        take(0, 8 * pair, 8)
        take(1, 4 * x, 4)
        take(1, 4 * x3, 4)
        yield next(times)
        a1.wait_recv()
        add_into(spot(ga, 4 * x1, 4), rx1.at[k, 0, pl.ds(4 * lax.rem(x1, 2), 4)])
        a3 = remote(spot(ga, 4 * x1, 4), rx2.at[k, 0], {"x": x1})
        b2.wait_recv()
        add_into(spot(gb, 4 * x3, 4), rx1.at[k, 1, pl.ds(4, 4)])
        b3 = remote(spot(gb, 4 * x3, 4), rx2.at[k, 1], {"x": x3})
        add_into(spot(ga, 4 * x, 4), rx1.at[k, 0, pl.ds(4 * lax.rem(x, 2), 4)])
        b1.wait_recv()
        add_into(spot(gb, 4 * x, 4), rx1.at[k, 1, pl.ds(0, 4)])
        yield next(times)
        a3.wait_recv()
        add_into(spot(ga, 4 * x, 4), rx2.at[k, 0])
        b3.wait_recv()
        add_into(spot(gb, 4 * x, 4), rx2.at[k, 1])
        over_z = [
            remote(coded.at[pl.ds(g, 2), 4 * x + zs[d]], rz.at[k, d - 1], {"z": zs[d]}) for d in (1, 2, 3)
        ]
        yield next(times)
        for copy in over_z:
            copy.wait_recv()
        if k == 0:
            got_momentum.wait_recv()
        replicas = 32.0
        for ab in range(2):
            summed = coded[g + ab, mine].astype(F32)
            for d in range(3):
                summed = summed + rz[k, d, ab].astype(F32)
            averaged = summed / replicas
            all_rows = pl.ds(group_rows(g + ab), rc)
            half_at = pl.ds((k * 2 + ab) * rc, rc)
            moved = momentum_keep * (mom[all_rows] + mom_in[half_at]) + averaged
            stepped = mas_in[half_at] - outer_rate * (averaged + momentum_keep * moved)
            nmom[all_rows] = moved
            nmas[all_rows] = stepped
            fresh[g + ab, mine] = stepped.astype(BF16)
        news = gather_start(fresh, k)
        chunk_rows = pl.ds(group_rows(g), 2 * rc)
        got_nmas = remote(nmas.at[chunk_rows], nmas.at[chunk_rows], {"c": 1 - c})
        got_nmom = remote(nmom.at[chunk_rows], nmom.at[chunk_rows], {"c": 1 - c})
        yield from gather(fresh, k, news, [next(times) for _ in range(4)])
        for first in (g, other):
            start = group_rows(first)

            @pl.loop(0, 2 * rc // tile)
            def _(i):
                at = pl.multiple_of(start + i * tile, tile)
                group = first + lax.div(i, rc // tile)
                here = pl.ds(pl.multiple_of(lax.rem(i, rc // tile) * tile, tile), tile)
                for b in range(blocks):
                    lanes = slice(b * BLOCK, (b + 1) * BLOCK)
                    old = wv[pl.ds(at, tile), lanes].astype(F32)
                    new = fresh[group, b, here, :].astype(F32)
                    merged[pl.ds(at, tile), lanes] = (mix_share * old + (1.0 - mix_share) * new).astype(BF16)

            span = pl.ds(start, 2 * rc)
            puts.append(local(merged.at[span], new_local.at[span]))
        yield next(times)
        got_nmas.wait_recv()
        got_nmom.wait_recv()
        for first in (g, other):
            span = pl.ds(group_rows(first), 2 * rc)
            puts.append(local(nmas.at[span], new_master.at[span]))
            puts.append(local(nmom.at[span], new_momentum.at[span]))

    def hidden_sends(dz):
        copies = {}
        for d in (2, 1, 3, 0):
            if dz == 0 and d == 0:
                continue
            to_z = (1 - zh) if dz else zh
            span = pl.ds(pl.multiple_of((to_z * 4 + ys[d]) * depth, depth), depth)
            target = {"zh": to_z, "y": ys[d]} if dz else {"y": ys[d]}
            copies[d] = remote(hidden.at[:, span], hr.at[dz, d], target)
        return copies

    half_columns = columns // 2
    step = 256
    tokens = hr.shape[2]

    def product(dz, d, count, side, write):
        left = hr[dz, pl.ds(d, count)].reshape(count * tokens, depth)

        @pl.loop(0, half_columns // step)
        def _(i):
            at = pl.multiple_of(i * step, step)
            right = wv[:, pl.ds(pl.multiple_of(side * half_columns + at, step), step)]
            write(pl.ds(at, step), jnp.dot(left, right, preferred_element_type=F32))

    def project(dz, arrived, times):
        times = iter(times)
        yield next(times)
        if dz == 0:
            in_hidden.wait()
        for d in (2, 1, 3, 0):
            if d in arrived:
                arrived[d].wait_recv()

        def store(side):
            def write(at, value):
                ps1[dz, side, :, :, at] = value.reshape(2, tokens, step).astype(BF16)
            return write

        product(dz, 1, 2, 0, store(0))
        left1 = remote(ps1.at[dz, 0], pr1.at[dz, 0], {"y": ys[1]})
        product(dz, 2, 2, 1, store(1))
        right1 = remote(ps1.at[dz, 1], pr1.at[dz, 1], {"y": ys[3]})

        yield next(times)

        def joined(side, slot):
            def write(at, value):
                ps2[dz, side, :, at] = (value + pr1[dz, side, slot, :, at].astype(F32)).astype(BF16)
            return write

        left1.wait_recv()
        product(dz, 3, 1, 0, joined(0, 1))
        left2 = remote(ps2.at[dz, 0], pr2.at[dz, 0], {"y": ys[3]})
        right1.wait_recv()
        product(dz, 1, 1, 1, joined(1, 0))
        right2 = remote(ps2.at[dz, 1], pr2.at[dz, 1], {"y": ys[1]})

        def keep(side, slot):
            def write(at, value):
                kept[dz, side, :, at] = value + pr1[dz, side, slot, :, at].astype(F32)
            return write

        product(dz, 0, 1, 0, keep(0, 0))
        product(dz, 0, 1, 1, keep(1, 1))
        yield next(times)
        left2.wait_recv()
        right2.wait_recv()
        if dz == 1:
            for side in range(2):
                psz[side] = (kept[1, side] + pr2[1, side].astype(F32)).astype(BF16)
            crossed = remote(psz, prz, {"zh": 1 - zh})
            yield next(times)
            crossed.wait_recv()
            for side in range(2):
                total = kept[0, side] + pr2[0, side].astype(F32) + prz[side].astype(F32)
                kv[:, side * half_columns:(side + 1) * half_columns] = total.astype(BF16)
            puts.append(local(kv, key_values))

    in_momentum.wait()
    got_momentum = remote(mom.at[other_rows], mom_in, {"c": 1 - c})
    got_master.wait_recv()
    mas_in[...] = mas_in[...] + mas[my_rows]
    for k in range(NC):
        for ab in range(2):
            held[first_group(c, k) + ab, mine] = mas_in[(k * 2 + ab) * rc:(k * 2 + ab + 1) * rc].astype(BF16)
    anchors = [gather_start(held, k) for k in range(NC)]
    crossing = hidden_sends(1)
    beside = hidden_sends(0)
    in_weights.wait()
    in_dither.wait()

    runs = [chunk(k, CHUNK_TIMES[k]) for k in range(NC)]
    runs += [project(0, beside, NEAR_TIMES), project(1, crossing, FAR_TIMES)]
    due = [(next(run), i, run) for i, run in enumerate(runs)]
    while due:
        due.sort(key=lambda entry: entry[:2])
        _, i, run = due.pop(0)
        when = next(run, None)
        if when is not None:
            due.append((when, i, run))
    for copy in sends:
        copy.wait_send()
    for copy in puts:
        copy.wait()


CHUNK_TIMES = [
    [12, 16, 23, 25, 33, 42, 47, 54, 61, 66, 73, 75, 76],
    [18, 24, 32, 36, 46, 56, 61, 69, 76, 81, 88, 90, 91],
]
NEAR_TIMES = [30, 44, 52]
FAR_TIMES = [58, 72, 78, 101]


def shards(hidden, local_weight, master, momentum, dither):
    weights = local_weight[0]
    rows, columns = weights.shape
    tokens, width = hidden.shape
    lanes = master.shape[1]
    core = lax.axis_index("c")
    blocks = columns // BLOCK
    groups = 4 * NC
    rc = rows // groups
    depth = width // 8

    def widened(part):
        low = jnp.pad(part, ((0, 0), (0, lanes)))
        high = jnp.pad(part, ((0, 0), (lanes, 0)))
        return jnp.where(core == 0, low, high)

    def narrowed(part):
        return jnp.where(core == 0, part[:, :lanes], part[:, lanes:])

    hbm = pl.BlockSpec(memory_space=pl.ANY)
    vm = pltpu.VMEM
    half = columns // 2
    scratch = [
        vm((rows, columns), BF16),
        vm((rows, blocks), jnp.int32),
        vm((rows, BLOCK), F32),
        vm((rows, BLOCK), F32),
        vm((rows // 2, BLOCK), F32),
        vm((rows // 2, BLOCK), F32),
        vm((rows, BLOCK), F32),
        vm((rows, BLOCK), F32),
        vm((groups, blocks, rc, BLOCK), BF16),
        vm((groups, blocks, rc, BLOCK), BF16),
        vm((NC, 2, blocks, rc, BLOCK), BF16),
        vm((NC, 2, 8, rc, BLOCK), BF16),
        vm((NC, 2, 4, rc, BLOCK), BF16),
        vm((NC, 3, 2, rc, BLOCK), BF16),
        vm((groups, blocks, rc, BLOCK), BF16),
        vm((rows, columns), BF16),
        vm((2, 4, tokens, depth), BF16),
        vm((2, 2, 2, tokens, half), BF16),
        vm((2, 2, 2, tokens, half), BF16),
        vm((2, 2, tokens, half), BF16),
        vm((2, 2, tokens, half), BF16),
        vm((2, tokens, half), BF16),
        vm((2, tokens, half), BF16),
        vm((2, 2, tokens, half), F32),
        vm((tokens, columns), BF16),
        pltpu.SemaphoreType.DMA((24 + 48 * NC,)),
        pltpu.SemaphoreType.DMA((24 + 48 * NC,)),
        pltpu.SemaphoreType.DMA((8 + 8 * NC,)),
    ]
    key_values, wide_master, wide_momentum, new_local = pl.pallas_call(
        kernel,
        out_shape=(
            jax.ShapeDtypeStruct((tokens, columns), BF16),
            jax.ShapeDtypeStruct((rows, BLOCK), F32),
            jax.ShapeDtypeStruct((rows, BLOCK), F32),
            jax.ShapeDtypeStruct((rows, columns), BF16),
        ),
        in_specs=[hbm] * 5,
        out_specs=[hbm] * 4,
        scratch_shapes=scratch,
        compiler_params=pltpu.CompilerParams(
            collective_id=0, has_side_effects=True, vmem_limit_bytes=60 * 1024 * 1024
        ),
        name="outer_step",
    )(hidden, weights, dither[0], widened(master), widened(momentum))
    return key_values, narrowed(wide_master), narrowed(wide_momentum), new_local[None]


def solution(mesh):
    finer = Mesh(mesh.devices.reshape(4, 4, 2, 2, 4), REP_FSDP)
    in_specs = (P(REP_FSDP, None), P(REP, FSDP, None), P(FSDP, REP), P(FSDP, REP), P(REP, FSDP, None))
    out_specs = (P(REP_FSDP, None), P(FSDP, REP), P(FSDP, REP), P(REP, FSDP, None))
    return jax.shard_map(shards, mesh=finer, in_specs=in_specs, out_specs=out_specs, check_vma=False)
```

time: 561 us -> 196 us (0.35)
  waiting for transfers between devices: 247 us -> 0 us
  Pallas kernels: 0 us -> 180 us
  blocking collectives: 170 us -> 0 us
  other arithmetic: 55.9 us -> 3.92 us
  local copies, waits for them, and re-layouts: 50.1 us -> 11.5 us
  matrix products: 13.7 us -> 0 us
  between operations: 14.2 us -> 0.68 us
  starting transfers between devices: 6.71 us -> 0 us
    all_gather x2 -> x0, waiting for transfers between devices: 207 us -> none  [stacked_from(): parts = lax.all_gather(parts, axes[k], axis=0, tiled=True)]
    pallas_call x0 -> x1, Pallas kernels: none -> 180 us  [shards(): pl.pallas_call(kernel, out_shape=(jax.ShapeDtypeStruct((tokens, columns),...]
    all_to_all x4 -> x0, blocking collectives: 170 us -> none  [the longest x1 100 us: shards(): lax.all_to_all(coded, REP, split_axis=1, concat_axis=0, tiled=True)]
    convert_element_type x6 -> x0, other arithmetic: 44.9 us -> none  [the longest x1 31.6 us: shards(): coded = code_block(delta, dither[0]).astype(jnp.bfloat16)]
    all_to_all x1 -> x0, waiting for transfers between devices: 39.9 us -> none  [sent_to_all(): return lax.all_to_all(copies, axis, split_axis=0, concat_axis=0, tiled=True)]
    transpose x1 -> x0, local copies, waits for them, and re-layouts: 23 us -> none  [stacked_from(): parts.transpose(*turned, *range(len(order), parts.ndim))]
    dot_general x1 -> x0, matrix products: 13.7 us -> none  [shards(): jnp.dot(hidden, gathered_by_axis(weights, FSDP, (0, 1), 0), preferred_ele...]
    reduce_max x2 -> x0, other arithmetic: 10.1 us -> none  [code_block(): scaling = (jnp.max(jnp.abs(blocked), axis=2, keepdims=True) + 1e-06) / 7.0]
  transfers between devices with their start and end apart: 3 -> 0, of which waited for: 2 -> 0; matrix products, arithmetic and copies ran while one was open for 15% -> 0% of each run, Pallas kernels for 0% -> 0%
where the time goes in v1:
time: 196 us
  Pallas kernels  180 us (92%)
  local copies, waits for them, and re-layouts  11.5 us (6%)
  other arithmetic  3.92 us (2%)
    pallas_call x1, Pallas kernels, shards(): pl.pallas_call(kernel, out_shape=(jax.ShapeDtypeStruct((tokens, columns),...  180 us
    unnamed x9, local copies, waits for them, and re-layouts  11.5 us

profile of v1, /device:TPU:41, one launch (start us, length us, event | category | flops | bytes accessed | tf_op | source)
XLA Modules:
  0.0 196.1 jit_solution(5140945543499163938)
XLA Ops:
  0.6 1.1 copy.10
  1.8 1.0 pad_select_fusion.1.master
  2.8 1.1 copy.12
  3.9 1.0 pad_select_fusion.momentum
  4.9 1.8 copy.9
  6.8 180.1 %outer_step.1 = (bf16[128,2048]{1,0:T(8,128)(2,1)}, f32[1024,128]{1,0:T(8,128)}, f32[1024,128]{1,0:T(8,128)}, bf16[1024,2048]{1,0:T(8,128)(2,1)}) custom-call(bf16[128,8192]{1,0:T(8,128)(2,1)} %hidden.1, bf16[1024,2048]{1,0:T(8,128)(2,1)} %bitcast.4, s32[1024,16]{1,0:T(8,128)} %bitcast.5, f32[1024,128]{1,0:T(8,128)} %pad_select_fusion.1.master, ...), custom_call_target="tpu_custom_call" | custom-call | tf_op jit(solution)/shard_map/outer_step/pallas_call | solution.py:445
  186.8 0.0 copy-start
  186.9 1.9 slice_select_fusion
  188.8 0.9 copy.15
  189.7 0.9 copy.14
  190.5 0.0 copy-done
  190.5 0.8 copy.18
  191.3 4.8 %copy.19 = bf16[1,1024,2048]{2,1,0:T(8,128)(2,1)} copy(bf16[1,1024,2048]{2,1,0:T(8,128)(2,1)} %bitcast.3) | data formatting | bytes 8388608
Async XLA Ops:
  186.8 3.7 %copy-start = (bf16[128,2048]{1,0:T(8,128)(2,1)S(1)}, bf16[128,2048]{1,0:T(8,128)(2,1)}, u32[]{:S(2)}) copy-start(bf16[128,2048]{1,0:T(8,128)(2,1)} %get-tuple-element.22) | copy-start | bytes 1572868

commit v2 on v1

v2 whole, which is shorter than its diff:
```python
import functools

import jax
import jax.numpy as jnp
from jax import lax
from jax.experimental import pallas as pl
from jax.experimental.pallas import tpu as pltpu
from jax.sharding import Mesh
from jax.sharding import PartitionSpec as P

BLOCK = 128
FSDP = ("zh", "y")
REP = ("x", "z", "c")
REP_FSDP = ("x", "z", "c", "zh", "y")
MESH = pl.DeviceIdType.MESH

momentum_keep = 0.9
outer_rate = 0.7
mix_share = 0.5

NC = 4
FAR = 2
SUB = 2
RET = 4
ORDER = [-1, -1, 0, -1, 1, 0, 0, 4, -1, 2, 1, 1, -1, 3, 0, -1, 0, -1, 1, -1, 2, 0, 1, -1, 2, 3, 3, 4, 4, -1, 1, 0, 2, -1, 2, -1, 1, 3, -1, 0, 2, 3, 1, 4, 5, 3, 2, -1, -1, 3, -1, 5, 2, 5, 3, 0, 1, 5, -1, -1, 2, 6, 3, 0, -1, 1, 6, 0, 0, -1, 6, 1, 1, 0, 6, -1, -1, 2, 1, 0, 0, -1, 1, 1, 3, 2, 2, -1, 3, 3, 2, 5, 3, 2, 2, 3, 3, 6]
F32 = jnp.float32
BF16 = jnp.bfloat16

SINC = (0.9999999993, -6.579735975, 12.98786004, -12.20766404, 6.688634018, -2.371384249, 0.5153655921)


def sine_share(levels):
    turn = levels - jnp.round(levels)
    square = turn * turn
    series = jnp.full_like(square, SINC[-1])
    for coefficient in SINC[-2::-1]:
        series = series * square + coefficient
    return turn * series


def kernel(
    hidden, weights, dither, master, momentum,
    key_values, new_master, new_momentum, new_local,
    wv, dv, narrow, offsets, mas_t, mom_t, mas, mom, turned,
    held, coded, paired, rx1, rx2, rz, fresh,
    hr, ps1, pr1, ps2, pr2, psz, prz, kept,
    send_sem, recv_sem, local_sem,
):
    rows, columns = wv.shape
    blocks = columns // BLOCK
    lanes = BLOCK // 2
    groups, _, rc, _ = held.shape
    x, z, c = lax.axis_index("x"), lax.axis_index("z"), lax.axis_index("c")
    zh, y = lax.axis_index("zh"), lax.axis_index("y")

    def flips(i):
        return i, i + 1 - 2 * lax.rem(i, 2), lax.rem(i + 2, 4), 3 - i

    xs, zs, ys = flips(x), flips(z), flips(y)
    x1, x3 = xs[1], xs[3]
    mine = x * 4 + z
    pair = lax.div(x, 2)
    partner = {"c": 1 - c}

    counts = {"remote": 0, "local": 0}
    sends = []
    finished = []

    def remote(src, dst, target):
        i = counts["remote"]
        counts["remote"] += 1
        copy = pltpu.make_async_remote_copy(
            src_ref=src, dst_ref=dst, send_sem=send_sem.at[i], recv_sem=recv_sem.at[i],
            device_id=target, device_id_type=MESH,
        )
        copy.start()
        sends.append(copy)
        return copy

    def local(src, dst):
        i = counts["local"]
        counts["local"] += 1
        copy = pltpu.make_async_copy(src, dst, local_sem.at[i])
        copy.start()
        return copy

    half_rows = rows // 2
    my_rows = pl.ds(pl.multiple_of(c * half_rows, half_rows), half_rows)
    other_rows = pl.ds(pl.multiple_of((1 - c) * half_rows, half_rows), half_rows)
    my_lanes = pl.ds(pl.multiple_of(c * lanes, lanes), lanes)
    depth = hr.shape[3]
    tokens = hr.shape[2]
    in_master = local(master.at[:, my_rows], mas_t.at[my_lanes])
    in_dither = local(dither, dv)
    in_weights = local(weights, wv)
    in_momentum = local(momentum.at[:, my_rows], mom_t.at[my_lanes])
    own_columns = pl.ds(pl.multiple_of((zh * 4 + y) * depth, depth), depth)
    in_hidden = local(hidden.at[:, own_columns], hr.at[0, 0])

    barrier = pltpu.get_barrier_semaphore()
    peers = [partner, {"x": x1}, {"x": x3}]
    peers += [{"z": zs[d]} for d in (1, 2, 3)]
    peers += [{"y": ys[d]} for d in (1, 2, 3)]
    peers += [{"zh": 1 - zh, "y": ys[d]} for d in range(4)]
    for peer in peers:
        pl.semaphore_signal(barrier, inc=1, device_id=peer, device_id_type=MESH)
    pl.semaphore_wait(barrier, len(peers))

    got_master = remote(master.at[:, other_rows], mas_t.at[my_lanes], partner)
    got_momentum = remote(momentum.at[:, other_rows], mom_t.at[my_lanes], partner)

    def first_group(half, k):
        return (half * NC + k) * 2

    def group_rows(group):
        return pl.multiple_of(group * rc, rc)

    def gather_start(buffer, k):
        piece = buffer.at[pl.ds(first_group(c, k), 2), mine]
        return [remote(piece, piece, {"z": zs[d]}) for d in (1, 2, 3)]

    def gather(buffer, k, over_z, between=None):
        g = first_group(c, k)

        def pass_on(part):
            return remote(part, part, partner)

        def part(ab, first, count):
            return buffer.at[g + ab, pl.ds(first, count)]

        yield
        for copy in over_z:
            copy.wait_recv()
        own_a, own_b = part(0, 4 * x, 4), part(1, 4 * x, 4)
        a1 = remote(own_a, own_a, {"x": x1})
        b1 = remote(own_b, own_b, {"x": x3})
        b2 = remote(own_b, own_b, {"x": x1})
        a2 = remote(own_a, own_a, {"x": x3})
        passed = [pass_on(buffer.at[pl.ds(g, 2), pl.ds(4 * x, 4)])]
        yield
        a1.wait_recv()
        far_a = part(0, 4 * x1, 4)
        a3 = remote(far_a, far_a, {"x": x3})
        passed.append(pass_on(far_a))
        yield
        b1.wait_recv()
        far_b = part(1, 4 * x3, 4)
        b3 = remote(far_b, far_b, {"x": x1})
        passed.append(pass_on(far_b))
        yield
        a2.wait_recv()
        a3.wait_recv()
        passed.append(pass_on(part(0, 8 * (1 - pair), 8)))
        b2.wait_recv()
        passed.append(pass_on(part(1, 4 * x1, 4)))
        b3.wait_recv()
        passed.append(pass_on(part(1, 4 * xs[2], 4)))
        if between is not None:
            between()
        yield
        for copy in passed:
            copy.wait_recv()

    tile = 16

    def code_groups(first):
        start = group_rows(first)
        part = blocks // 2
        count = 2 * (2 * rc // tile)

        def place(i):
            row = lax.div(i, 2) * tile
            at = pl.ds(pl.multiple_of(start + row, tile), tile)
            here = pl.ds(pl.multiple_of(lax.rem(row, rc), tile), tile)
            return at, first + lax.div(row, rc), here, lax.rem(i, 2) * part

        def delta_of(spot, b):
            at, group, here, low = spot
            old = wv[at, pl.ds(pl.multiple_of((low + b) * BLOCK, BLOCK), BLOCK)].astype(F32)
            return held[group, low + b, here, :].astype(F32) - old

        def scalings(i):
            spot = place(i)
            found = []
            for b in range(part):
                largest = jnp.max(jnp.abs(delta_of(spot, b)), axis=1, keepdims=True)
                found.append(jnp.broadcast_to((largest + 1e-06) / 7.0, (tile, BLOCK)))
            return tuple(found)

        def body(i, scales):
            spot = place(i)
            ahead = scalings(jnp.minimum(i + 1, count - 1))
            _, group, here, low = spot
            for b in range(part):
                scaling = scales[b]
                offset = offsets[group, low + b, here, :]
                levels = jnp.clip(delta_of(spot, b) * (1.0 / scaling) + offset, -8.0, 7.0)
                smooth = levels - sine_share(levels)
                coded[group, low + b, here, :] = (scaling * (smooth - offset)).astype(BF16)
            return ahead

        lax.fori_loop(0, count, body, scalings(0))

    def merge_groups(first):
        start = group_rows(first)

        @pl.loop(0, 2 * rc // tile)
        def _(i):
            at = pl.multiple_of(start + i * tile, tile)
            group = first + lax.div(i, rc // tile)
            here = pl.ds(pl.multiple_of(lax.rem(i, rc // tile) * tile, tile), tile)
            for b in range(blocks):
                span = slice(b * BLOCK, (b + 1) * BLOCK)
                old = wv[pl.ds(at, tile), span].astype(F32)
                new = fresh[group, b, here, :].astype(F32)
                new_local[pl.ds(at, tile), span] = (mix_share * old + (1.0 - mix_share) * new).astype(BF16)


    def add_into(target, source):
        step = 64 if rc % 64 == 0 else rc

        @pl.loop(0, source.shape[0] * (rc // step))
        def _(i):
            at = (lax.div(i, rc // step), pl.ds(pl.multiple_of(lax.rem(i, rc // step) * step, step), step))
            target[at] = (target[at].astype(F32) + source[at].astype(F32)).astype(BF16)

    def chunk(k):
        g, other = first_group(c, k), first_group(1 - c, k)
        yield from gather(held, k, anchors[k], lambda: code_groups(g))
        code_groups(other)
        got = remote(coded.at[pl.ds(other, 2)], paired.at[k], partner)
        yield
        got.wait_recv()
        ga, gb = g, g + 1

        def spot(group, first, count):
            return coded.at[group, pl.ds(first, count)]

        def take(ab, first, count):
            add_into(spot(g + ab, first, count), paired.at[k, ab, pl.ds(first, count)])

        away = 8 * (1 - pair)
        take(0, away, 8)
        a1 = remote(spot(ga, away, 8), rx1.at[k, 0], {"x": x3})
        take(1, 4 * x1, 4)
        b1 = remote(spot(gb, 4 * x1, 4), rx1.at[k, 1, pl.ds(0, 4)], {"x": x1})
        take(1, 4 * xs[2], 4)
        b2 = remote(spot(gb, 4 * xs[2], 4), rx1.at[k, 1, pl.ds(4, 4)], {"x": x1})
        take(0, 8 * pair, 8)
        take(1, 4 * x, 4)
        take(1, 4 * x3, 4)
        yield
        a1.wait_recv()
        add_into(spot(ga, 4 * x1, 4), rx1.at[k, 0, pl.ds(4 * lax.rem(x1, 2), 4)])
        a3 = remote(spot(ga, 4 * x1, 4), rx2.at[k, 0], {"x": x1})
        b2.wait_recv()
        add_into(spot(gb, 4 * x3, 4), rx1.at[k, 1, pl.ds(4, 4)])
        b3 = remote(spot(gb, 4 * x3, 4), rx2.at[k, 1], {"x": x3})
        add_into(spot(ga, 4 * x, 4), rx1.at[k, 0, pl.ds(4 * lax.rem(x, 2), 4)])
        b1.wait_recv()
        add_into(spot(gb, 4 * x, 4), rx1.at[k, 1, pl.ds(0, 4)])
        yield
        a3.wait_recv()
        add_into(spot(ga, 4 * x, 4), rx2.at[k, 0])
        b3.wait_recv()
        add_into(spot(gb, 4 * x, 4), rx2.at[k, 1])
        over_z = [
            remote(coded.at[pl.ds(g, 2), 4 * x + zs[d]], rz.at[k, d - 1], {"z": zs[d]}) for d in (1, 2, 3)
        ]
        yield
        for copy in over_z:
            copy.wait_recv()
        replicas = 32.0
        for ab in range(2):
            summed = coded[g + ab, mine].astype(F32)
            for d in range(3):
                summed = summed + rz[k, d, ab].astype(F32)
            averaged = summed / replicas
            at = pl.ds((k * 2 + ab) * rc, rc)
            moved = momentum_keep * mom[at] + averaged
            stepped = mas[at] - outer_rate * (averaged + momentum_keep * moved)
            mom[at] = moved
            mas[at] = stepped
            fresh[g + ab, mine] = stepped.astype(BF16)
        news = gather_start(fresh, k)
        span = pl.ds(k * 2 * rc, 2 * rc)
        place = pl.ds(pl.multiple_of(c * half_rows + k * 2 * rc, 2 * rc), 2 * rc)
        theirs = pl.ds(pl.multiple_of((1 - c) * lanes, lanes), lanes)
        back = []
        for which, (values, out) in enumerate(((mas, new_master), (mom, new_momentum))):
            turned[which, :, span] = values[span].T
            back.append(remote(turned.at[which, theirs, span], out.at[:, place], partner))
            out[:, place] = turned[which, my_lanes, span]
        yield from gather(fresh, k, news, lambda: merge_groups(g))
        merge_groups(other)
        yield
        for copy in back:
            copy.wait_recv()

    waiting = []

    def hidden_send(dz, d, first, count):
        here = pl.ds(first, count)
        to_z = (1 - zh) if dz else zh
        span = pl.ds(pl.multiple_of((to_z * 4 + ys[d]) * depth, depth), depth)
        target = {"zh": to_z, "y": ys[d]} if dz else {"y": ys[d]}
        return remote(hidden.at[here, span], hr.at[dz, d, here], target)

    def later(copies, start):
        waiting.append(lambda: copies.append(start()))

    half_columns = columns // 2
    step = 512

    def project(dz, first, count, arrived):
        here = pl.ds(first, count)
        yield
        if dz == 0:
            in_hidden.wait()
        assert len(arrived) == (4 * SUB if dz else 3)
        for copy in arrived:
            copy.wait_recv()

        def products(side, away, stay):
            @pl.loop(0, half_columns // step)
            def _(i):
                at = pl.multiple_of(i * step, step)
                left = hr[dz, :, here].reshape(4 * count, depth)
                right = wv[:, pl.ds(pl.multiple_of(side * half_columns + at, step), step)]
                result = jnp.dot(left, right, preferred_element_type=F32)
                for n in range(2):
                    d = away[n]
                    ps1[dz, side, n, here, pl.ds(at, step)] = result[d * count:(d + 1) * count].astype(BF16)
                    d = stay[n]
                    kept[dz, side, n, here, pl.ds(at, step)] = result[d * count:(d + 1) * count]

        products(0, (1, 2), (0, 3))
        left1 = remote(ps1.at[dz, 0, :, here], pr1.at[dz, 0, :, here], {"y": ys[1]})
        products(1, (2, 3), (0, 1))
        right1 = remote(ps1.at[dz, 1, :, here], pr1.at[dz, 1, :, here], {"y": ys[3]})
        yield
        left1.wait_recv()
        ps2[dz, 0, here] = (kept[dz, 0, 1, here] + pr1[dz, 0, 1, here].astype(F32)).astype(BF16)
        left2 = remote(ps2.at[dz, 0, here], pr2.at[dz, 0, here], {"y": ys[3]})
        yield
        right1.wait_recv()
        ps2[dz, 1, here] = (kept[dz, 1, 1, here] + pr1[dz, 1, 0, here].astype(F32)).astype(BF16)
        right2 = remote(ps2.at[dz, 1, here], pr2.at[dz, 1, here], {"y": ys[1]})
        yield
        left2.wait_recv()
        right2.wait_recv()
        for side in range(2):
            total = kept[dz, side, 0, here] + pr1[dz, side, side, here].astype(F32)
            total = total + pr2[dz, side, here].astype(F32)
            if dz == 1:
                psz[side, here] = total.astype(BF16)
            else:
                kept[dz, side, 0, here] = total
        if dz == 0:
            finished.append("near")
        else:
            crossed = []
            for r in range(RET):
                part = pl.ds(r * (half_columns // RET), half_columns // RET)
                later(crossed, lambda part=part: remote(
                    psz.at[:, here, part], prz.at[:, here, part], {"zh": 1 - zh}))
            yield
            assert len(crossed) == RET
            for copy in crossed:
                copy.wait_recv()
            assert "near" in finished
            for side in range(2):
                total = kept[0, side, 0, here] + prz[side, here].astype(F32)
                key_values[here, side * half_columns:(side + 1) * half_columns] = total.astype(BF16)

    beside = [hidden_send(0, d, 0, tokens) for d in (2, 1, 3)]
    in_master.wait()
    got_master.wait_recv()
    for k in range(NC):
        span = pl.ds(k * 2 * rc, 2 * rc)
        mas[span] = mas_t[:, span].T
        for ab in range(2):
            held[first_group(c, k) + ab, mine] = mas[(k * 2 + ab) * rc:(k * 2 + ab + 1) * rc].astype(BF16)
    anchors = [gather_start(held, k) for k in range(NC)]
    share = tokens // FAR
    crossing = [[] for r in range(FAR)]
    piece = share // SUB
    for r in range(FAR):
        for j in range(SUB):
            for d in (2, 1, 3, 0):
                later(crossing[r], lambda d=d, at=r * share + j * piece: hidden_send(1, d, at, piece))
    in_momentum.wait()
    got_momentum.wait_recv()
    for k in range(NC):
        span = pl.ds(k * 2 * rc, 2 * rc)
        mom[span] = mom_t[:, span].T
    in_dither.wait()
    for k in range(rows // BLOCK):
        span = pl.ds(k * BLOCK, BLOCK)
        narrow[span] = ((dv[:, span].astype(F32) + 0.5) / 16.0 - 0.5).T

    @pl.loop(0, rows // tile)
    def _(i):
        shift = narrow[pl.ds(pl.multiple_of(i * tile, tile), tile), :]
        group = lax.div(i, rc // tile)
        here = pl.ds(pl.multiple_of(lax.rem(i, rc // tile) * tile, tile), tile)
        for b in range(blocks):
            offsets[group, b, here, :] = jnp.broadcast_to(shift[:, b:b + 1], (tile, BLOCK))

    in_weights.wait()

    runs = [chunk(k) for k in range(NC)]
    runs.append(project(0, 0, tokens, beside))
    runs += [project(1, r * share, share, crossing[r]) for r in range(FAR)]
    for run in runs:
        next(run)
    live = list(range(len(runs)))
    for i in ORDER:
        if i < 0:
            waiting.pop(0)()
        elif next(runs[i], "end") == "end":
            live.remove(i)
    assert not live and not waiting
    for copy in sends:
        copy.wait_send()


def shards(hidden, local_weight, master, momentum, dither):
    weights = local_weight[0]
    rows, columns = weights.shape
    tokens, width = hidden.shape
    blocks = columns // BLOCK
    groups = 4 * NC
    rc = rows // groups
    depth = width // 8
    lanes = master.shape[1]
    hbm = pl.BlockSpec(memory_space=pl.ANY)
    vm = pltpu.VMEM
    half = columns // 2
    scratch = [
        vm((rows, columns), BF16),
        vm((blocks, rows), jnp.int32),
        vm((rows, blocks), F32),
        vm((groups, blocks, rc, BLOCK), F32),
        vm((BLOCK, rows // 2), F32),
        vm((BLOCK, rows // 2), F32),
        vm((rows // 2, BLOCK), F32),
        vm((rows // 2, BLOCK), F32),
        vm((2, BLOCK, rows // 2), F32),
        vm((groups, blocks, rc, BLOCK), BF16),
        vm((groups, blocks, rc, BLOCK), BF16),
        vm((NC, 2, blocks, rc, BLOCK), BF16),
        vm((NC, 2, 8, rc, BLOCK), BF16),
        vm((NC, 2, 4, rc, BLOCK), BF16),
        vm((NC, 3, 2, rc, BLOCK), BF16),
        vm((groups, blocks, rc, BLOCK), BF16),
        vm((2, 4, tokens, depth), BF16),
        vm((2, 2, 2, tokens, half), BF16),
        vm((2, 2, 2, tokens, half), BF16),
        vm((2, 2, tokens, half), BF16),
        vm((2, 2, tokens, half), BF16),
        vm((2, tokens, half), BF16),
        vm((2, tokens, half), BF16),
        vm((2, 2, 2, tokens, half), F32),
        pltpu.SemaphoreType.DMA((24 + 42 * NC + (4 + 4 * SUB + RET) * FAR,)),
        pltpu.SemaphoreType.DMA((24 + 42 * NC + (4 + 4 * SUB + RET) * FAR,)),
        pltpu.SemaphoreType.DMA((5,)),
    ]
    key_values, new_master, new_momentum, new_local = pl.pallas_call(
        kernel,
        out_shape=(
            jax.ShapeDtypeStruct((tokens, columns), BF16),
            jax.ShapeDtypeStruct((lanes, rows), F32),
            jax.ShapeDtypeStruct((lanes, rows), F32),
            jax.ShapeDtypeStruct((rows, columns), BF16),
        ),
        in_specs=[hbm] * 5,
        out_specs=[pl.BlockSpec(memory_space=pltpu.VMEM)] * 4,
        scratch_shapes=scratch,
        compiler_params=pltpu.CompilerParams(
            collective_id=0, has_side_effects=True, vmem_limit_bytes=46 * 1024 * 1024
        ),
        name="outer_step",
    )(hidden, weights, dither[0].T, master.T, momentum.T)
    return key_values, new_master.T, new_momentum.T, new_local[None]


def solution(mesh):
    finer = Mesh(mesh.devices.reshape(4, 4, 2, 2, 4), REP_FSDP)
    in_specs = (P(REP_FSDP, None), P(REP, FSDP, None), P(FSDP, REP), P(FSDP, REP), P(REP, FSDP, None))
    out_specs = (P(REP_FSDP, None), P(FSDP, REP), P(FSDP, REP), P(REP, FSDP, None))
    return jax.shard_map(shards, mesh=finer, in_specs=in_specs, out_specs=out_specs, check_vma=False)
```

time: 196 us -> 143 us (0.73)
  the two profiles are of different devices: /device:TPU:41 before, /device:TPU:73 now
where the time goes in v2:
time: 143 us
  Pallas kernels  134 us (94%)
  local copies, waits for them, and re-layouts  8.53 us (6%)
    pallas_call x1, Pallas kernels, shards(): pl.pallas_call(kernel, out_shape=(jax.ShapeDtypeStruct((tokens, columns),...  134 us
    unnamed x12, local copies, waits for them, and re-layouts  8.53 us

profile of v2, /device:TPU:73, one launch (start us, length us, event | category | flops | bytes accessed | tf_op | source)
XLA Modules:
  0.0 143.1 jit_solution(3244584576523667509)
XLA Ops:
  0.6 0.0 copy-start
  0.6 1.6 %copy-done = bf16[128,8192]{1,0:T(8,128)(2,1)S(1)} copy-done((bf16[128,8192]{1,0:T(8,128)(2,1)S(1)}, bf16[128,8192]{1,0:T(8,128)(2,1)}, u32[]{:S(2)}) %copy-start) | copy-done | bytes 2097176
  2.2 0.0 copy-start.1
  2.2 0.9 copy-done.1
  3.2 0.0 copy-start.2
  3.2 0.9 copy-done.2
  4.1 0.0 copy-start.3
  4.1 0.8 copy-done.3
  5.0 134.0 %outer_step.1 = (bf16[128,2048]{1,0:T(8,128)(2,1)S(1)}, f32[64,1024]{1,0:T(8,128)S(1)}, f32[64,1024]{1,0:T(8,128)S(1)}, bf16[1024,2048]{1,0:T(8,128)(2,1)S(1)}) custom-call(bf16[128,8192]{1,0:T(8,128)(2,1)S(1)} %copy-done, bf16[1024,2048]{1,0:T(8,128)(2,1)} %bitcast.15, s32[16,1024]{1,0:T(8,128)S(1)} %bitcast.14, f32[64,1024]{1,0:T(8,128)S(1)} %bitcast.12, ...), custom_call_target="tpu_custom_call" | custom-call | tf_op jit(solution)/shard_map/outer_step/pallas_call | solution.py:469
  138.9 0.8 copy.13
  139.7 0.7 copy.14
  140.4 0.7 copy.15
  141.1 2.0 %copy.16 = bf16[1,1024,2048]{2,1,0:T(8,128)(2,1)} copy(bf16[1,1024,2048]{2,1,0:T(8,128)(2,1)S(1)} %bitcast.9) | data formatting | bytes 8388608
Async XLA Ops:
  0.6 1.6 %copy-start = (bf16[128,8192]{1,0:T(8,128)(2,1)S(1)}, bf16[128,8192]{1,0:T(8,128)(2,1)}, u32[]{:S(2)}) copy-start(bf16[128,8192]{1,0:T(8,128)(2,1)} %hidden.1) | copy-start | bytes 6291460
  2.2 0.9 copy-start.1
  3.2 0.9 copy-start.2
  4.1 0.8 copy-start.3

commit v3 on v2

--- a/solution.py
+++ b/solution.py
@@ -22,7 +22,7 @@
 FAR = 2
 SUB = 2
 RET = 4
-ORDER = [-1, -1, 0, -1, 1, 0, 0, 4, -1, 2, 1, 1, -1, 3, 0, -1, 0, -1, 1, -1, 2, 0, 1, -1, 2, 3, 3, 4, 4, -1, 1, 0, 2, -1, 2, -1, 1, 3, -1, 0, 2, 3, 1, 4, 5, 3, 2, -1, -1, 3, -1, 5, 2, 5, 3, 0, 1, 5, -1, -1, 2, 6, 3, 0, -1, 1, 6, 0, 0, -1, 6, 1, 1, 0, 6, -1, -1, 2, 1, 0, 0, -1, 1, 1, 3, 2, 2, -1, 3, 3, 2, 5, 3, 2, 2, 3, 3, 6]
+ORDER = [-1, 0, 1, -1, 2, 3, 4, -1, 0, 1, -1, 0, 0, -1, 2, 3, 1, 1, -1, 0, -1, 0, -1, 2, 2, 3, 3, 4, 4, -1, 0, 1, -1, 1, -1, 2, -1, 0, 1, 2, -1, 3, 0, 2, 3, -1, 1, 4, 5, 3, -1, 2, 1, 0, 3, 2, 5, 5, 3, 1, 0, 5, 6, -1, 2, -1, 3, 1, 0, 6, 6, -1, 2, 0, 0, -1, 6, 3, 0, 1, -1, 0, 0, -1, 2, 1, 1, -1, 3, 2, 2, 5, -1, 1, 3, 3, 1, 1, 2, 3, 2, 2, 3, 3, 6]
 F32 = jnp.float32
 BF16 = jnp.bfloat16
 
@@ -117,7 +117,7 @@
 
     def gather_start(buffer, k):
         piece = buffer.at[pl.ds(first_group(c, k), 2), mine]
-        return [remote(piece, piece, {"z": zs[d]}) for d in (1, 2, 3)]
+        return [remote(piece, piece, {"z": zs[d]}) for d in (2, 1)]
 
     def gather(buffer, k, over_z, between=None):
         g = first_group(c, k)
@@ -129,8 +129,13 @@
             return buffer.at[g + ab, pl.ds(first, count)]
 
         yield
-        for copy in over_z:
-            copy.wait_recv()
+        far_z, near_z = over_z
+        far_z.wait_recv()
+        crossed = buffer.at[pl.ds(g, 2), 4 * x + zs[2]]
+        onward = remote(crossed, crossed, {"z": zs[1]})
+        yield
+        near_z.wait_recv()
+        onward.wait_recv()
         own_a, own_b = part(0, 4 * x, 4), part(1, 4 * x, 4)
         a1 = remote(own_a, own_a, {"x": x1})
         b1 = remote(own_b, own_b, {"x": x3})
@@ -374,6 +379,15 @@
                 key_values[here, side * half_columns:(side + 1) * half_columns] = total.astype(BF16)
 
     beside = [hidden_send(0, d, 0, tokens) for d in (2, 1, 3)]
+    share = tokens // FAR
+    crossing = [[] for r in range(FAR)]
+    piece = share // SUB
+    for r in range(FAR):
+        for j in range(SUB):
+            for d in (2, 1, 3, 0):
+                later(crossing[r], lambda d=d, at=r * share + j * piece: hidden_send(1, d, at, piece))
+    for _ in range(1):
+        waiting.pop(0)()
     in_master.wait()
     got_master.wait_recv()
     for k in range(NC):
@@ -382,13 +396,6 @@
         for ab in range(2):
             held[first_group(c, k) + ab, mine] = mas[(k * 2 + ab) * rc:(k * 2 + ab + 1) * rc].astype(BF16)
     anchors = [gather_start(held, k) for k in range(NC)]
-    share = tokens // FAR
-    crossing = [[] for r in range(FAR)]
-    piece = share // SUB
-    for r in range(FAR):
-        for j in range(SUB):
-            for d in (2, 1, 3, 0):
-                later(crossing[r], lambda d=d, at=r * share + j * piece: hidden_send(1, d, at, piece))
     in_momentum.wait()
     got_momentum.wait_recv()
     for k in range(NC):
@@ -481,7 +488,10 @@
             collective_id=0, has_side_effects=True, vmem_limit_bytes=46 * 1024 * 1024
         ),
         name="outer_step",
-    )(hidden, weights, dither[0].T, master.T, momentum.T)
+    )(*(
+        pltpu.with_memory_space_constraint(operand, pltpu.HBM)
+        for operand in (hidden, weights, dither[0].T, master.T, momentum.T)
+    ))
     return key_values, new_master.T, new_momentum.T, new_local[None]
 
 

time: 143 us -> 126 us (0.88)
  the two profiles are of different devices: /device:TPU:73 before, /device:TPU:1 now
where the time goes in v3:
time: 126 us
  Pallas kernels  121 us (96%)
  local copies, waits for them, and re-layouts  4.21 us (3%)
    pallas_call x1, Pallas kernels, shards(): pl.pallas_call(kernel, out_shape=(jax.ShapeDtypeStruct((tokens, columns),...  121 us
    unnamed x4, local copies, waits for them, and re-layouts  4.21 us

profile of v3, /device:TPU:1, one launch (start us, length us, event | category | flops | bytes accessed | tf_op | source)
XLA Modules:
  0.0 125.5 jit_solution(9515416187394943571)
XLA Ops:
  0.6 120.7 %outer_step.1 = (bf16[128,2048]{1,0:T(8,128)(2,1)S(1)}, f32[64,1024]{1,0:T(8,128)S(1)}, f32[64,1024]{1,0:T(8,128)S(1)}, bf16[1024,2048]{1,0:T(8,128)(2,1)S(1)}) custom-call(bf16[128,8192]{1,0:T(8,128)(2,1)} %hidden.1, bf16[1024,2048]{1,0:T(8,128)(2,1)} %bitcast.12, s32[16,1024]{1,0:T(8,128)} %bitcast.15, f32[64,1024]{1,0:T(8,128)} %bitcast.13, ...), custom_call_target="tpu_custom_call" | custom-call | tf_op jit(solution)/shard_map/outer_step/pallas_call | solution.py:476
  121.3 0.8 copy.13
  122.1 0.7 copy.14
  122.8 0.7 copy.15
  123.5 2.0 %copy.16 = bf16[1,1024,2048]{2,1,0:T(8,128)(2,1)} copy(bf16[1,1024,2048]{2,1,0:T(8,128)(2,1)S(1)} %bitcast.9) | data formatting | bytes 8388608

commit v4 on v3

--- a/solution.py
+++ b/solution.py
@@ -19,10 +19,10 @@
 mix_share = 0.5
 
 NC = 4
-FAR = 2
-SUB = 2
-RET = 4
-ORDER = [-1, 0, 1, -1, 2, 3, 4, -1, 0, 1, -1, 0, 0, -1, 2, 3, 1, 1, -1, 0, -1, 0, -1, 2, 2, 3, 3, 4, 4, -1, 0, 1, -1, 1, -1, 2, -1, 0, 1, 2, -1, 3, 0, 2, 3, -1, 1, 4, 5, 3, -1, 2, 1, 0, 3, 2, 5, 5, 3, 1, 0, 5, 6, -1, 2, -1, 3, 1, 0, 6, 6, -1, 2, 0, 0, -1, 6, 3, 0, 1, -1, 0, 0, -1, 2, 1, 1, -1, 3, 2, 2, 5, -1, 1, 3, 3, 1, 1, 2, 3, 2, 2, 3, 3, 6]
+FAR = 4
+SUB = 1
+RET = 2
+ORDER = [0, -1, -1, 2, 0, 1, -1, 3, -1, -1, -1, -1, 0, 0, -1, 1, 4, 2, -1, 0, 1, 1, 5, 3, 0, 2, -1, -1, -1, -1, 2, -1, 1, 0, 3, 3, 1, 2, 5, 1, 2, 0, 3, 2, 1, 0, -1, 3, 5, 6, 2, 1, 3, 5, 7, -1, 6, 2, 3, 4, 1, 0, 6, 3, 7, 7, 8, 2, 1, 4, -1, 0, 3, 2, 8, 6, 1, 8, -1, -1, 0, 1, 2, 3, 8, -1, -1, 7, 0, 1, 0, 3, 2, -1, -1, 4, 6, 5, 1, 2, 3, 3, 0, 0, 2, 3, 8, 1, 2, 2, 1, 3, 7, 3, 0]
 F32 = jnp.float32
 BF16 = jnp.bfloat16
 
@@ -119,7 +119,7 @@
         piece = buffer.at[pl.ds(first_group(c, k), 2), mine]
         return [remote(piece, piece, {"z": zs[d]}) for d in (2, 1)]
 
-    def gather(buffer, k, over_z, between=None):
+    def gather(buffer, k, over_z, early=None, between=None):
         g = first_group(c, k)
 
         def pass_on(part):
@@ -133,6 +133,8 @@
         far_z.wait_recv()
         crossed = buffer.at[pl.ds(g, 2), 4 * x + zs[2]]
         onward = remote(crossed, crossed, {"z": zs[1]})
+        if early is not None:
+            early()
         yield
         near_z.wait_recv()
         onward.wait_recv()
@@ -204,7 +206,18 @@
                 coded[group, low + b, here, :] = (scaling * (smooth - offset)).astype(BF16)
             return ahead
 
-        lax.fori_loop(0, count, body, scalings(0))
+        lax.fori_loop(0, count, body, scalings(0), unroll=2)
+
+    def spread_offsets(first):
+        start = group_rows(first)
+
+        @pl.loop(0, 2 * rc // tile)
+        def _(i):
+            shift = narrow[pl.ds(pl.multiple_of(start + i * tile, tile), tile), :]
+            group = first + lax.div(i, rc // tile)
+            here = pl.ds(pl.multiple_of(lax.rem(i, rc // tile) * tile, tile), tile)
+            for b in range(blocks):
+                offsets[group, b, here, :] = jnp.broadcast_to(shift[:, b:b + 1], (tile, BLOCK))
 
     def merge_groups(first):
         start = group_rows(first)
@@ -231,7 +244,11 @@
 
     def chunk(k):
         g, other = first_group(c, k), first_group(1 - c, k)
-        yield from gather(held, k, anchors[k], lambda: code_groups(g))
+        def spread():
+            spread_offsets(g)
+            spread_offsets(other)
+
+        yield from gather(held, k, anchors[k], spread, lambda: code_groups(g))
         code_groups(other)
         got = remote(coded.at[pl.ds(other, 2)], paired.at[k], partner)
         yield
@@ -296,7 +313,7 @@
             turned[which, :, span] = values[span].T
             back.append(remote(turned.at[which, theirs, span], out.at[:, place], partner))
             out[:, place] = turned[which, my_lanes, span]
-        yield from gather(fresh, k, news, lambda: merge_groups(g))
+        yield from gather(fresh, k, news, None, lambda: merge_groups(g))
         merge_groups(other)
         yield
         for copy in back:
@@ -405,14 +422,6 @@
     for k in range(rows // BLOCK):
         span = pl.ds(k * BLOCK, BLOCK)
         narrow[span] = ((dv[:, span].astype(F32) + 0.5) / 16.0 - 0.5).T
-
-    @pl.loop(0, rows // tile)
-    def _(i):
-        shift = narrow[pl.ds(pl.multiple_of(i * tile, tile), tile), :]
-        group = lax.div(i, rc // tile)
-        here = pl.ds(pl.multiple_of(lax.rem(i, rc // tile) * tile, tile), tile)
-        for b in range(blocks):
-            offsets[group, b, here, :] = jnp.broadcast_to(shift[:, b:b + 1], (tile, BLOCK))
 
     in_weights.wait()
 

time: 126 us -> 120 us (0.952)
  the two profiles are of different devices: /device:TPU:1 before, /device:TPU:41 now
where the time goes in v4:
time: 120 us; the launch traced here: 117 us
  Pallas kernels  113 us (94%)
  local copies, waits for them, and re-layouts  4.21 us (4%)
    pallas_call x1, Pallas kernels, shards(): pl.pallas_call(kernel, out_shape=(jax.ShapeDtypeStruct((tokens, columns),...  113 us
    unnamed x4, local copies, waits for them, and re-layouts  4.21 us

profile of v4, /device:TPU:41, one launch (start us, length us, event | category | flops | bytes accessed | tf_op | source)
XLA Modules:
  0.0 117.4 jit_solution(18329549451244875986)
XLA Ops:
  0.6 112.6 %outer_step.1 = (bf16[128,2048]{1,0:T(8,128)(2,1)S(1)}, f32[64,1024]{1,0:T(8,128)S(1)}, f32[64,1024]{1,0:T(8,128)S(1)}, bf16[1024,2048]{1,0:T(8,128)(2,1)S(1)}) custom-call(bf16[128,8192]{1,0:T(8,128)(2,1)} %hidden.1, bf16[1024,2048]{1,0:T(8,128)(2,1)} %bitcast.12, s32[16,1024]{1,0:T(8,128)} %bitcast.15, f32[64,1024]{1,0:T(8,128)} %bitcast.13, ...), custom_call_target="tpu_custom_call" | custom-call | tf_op jit(solution)/shard_map/outer_step/pallas_call | solution.py:485
  113.2 0.8 copy.13
  114.0 0.7 copy.14
  114.7 0.7 copy.15
  115.4 2.0 %copy.16 = bf16[1,1024,2048]{2,1,0:T(8,128)(2,1)} copy(bf16[1,1024,2048]{2,1,0:T(8,128)(2,1)S(1)} %bitcast.9) | data formatting | bytes 8388608
